TPU v7x, 16 devices: a 4x2x1 block of a 4x4x8 slice. The times are simulated.
16 devices in a mesh: rep: 2 (over y, z), dp: 8 (over x, core).
Axes of the slice: x: 4, y: 2, z: 1, core: 2. Of those that a mesh axis runs over, the one named last changes fastest.
The devices are a block of a 4x4x8 slice.
Arguments:
- x: bfloat16 [16, 2048, 896], P(('rep', 'dp')), parts along dimension 0
- dy: bfloat16 [16, 2048, 896], P(('rep', 'dp')), parts along dimension 0
- w_gate: bfloat16 [2, 896, 2560], P(None, 'dp')
- w_up: bfloat16 [2, 896, 2560], P(None, 'dp')
- w_down: bfloat16 [2, 2560, 896], P(None, 'dp')
- m_w_gate: float32 [2, 896, 2560], P(None, 'dp')
- m_w_up: float32 [2, 896, 2560], P(None, 'dp')
- m_w_down: float32 [2, 2560, 896], P(None, 'dp')
- v_w_gate: float32 [2, 896, 2560], P(None, 'dp')
- v_w_up: float32 [2, 896, 2560], P(None, 'dp')
- v_w_down: float32 [2, 2560, 896], P(None, 'dp')
Outputs:
- output 1: bfloat16 [4, 896, 2560], P('rep', 'dp'), parts along dimension 0
- output 2: bfloat16 [4, 896, 2560], P('rep', 'dp'), parts along dimension 0
- output 3: bfloat16 [4, 2560, 896], P('rep', 'dp'), parts along dimension 0
- output 4: float32 [4, 896, 2560], P('rep', 'dp'), parts along dimension 0
- output 5: float32 [4, 896, 2560], P('rep', 'dp'), parts along dimension 0
- output 6: float32 [4, 2560, 896], P('rep', 'dp'), parts along dimension 0
- output 7: float32 [4, 896, 2560], P('rep', 'dp'), parts along dimension 0
- output 8: float32 [4, 896, 2560], P('rep', 'dp'), parts along dimension 0
- output 9: float32 [4, 2560, 896], P('rep', 'dp'), parts along dimension 0
There are 2 independent parts. A program takes and returns all parts, laid end to end along the dimension named above; an argument that names none is the same for every part.
All inputs are finite; a program needn't handle non-finite values.
Results may differ from a plain program's by a relative error of at most 0.022.
Values are sent between devices in bfloat16 or wider.
A program may use at most 768 MiB of HBM per device.

v0:
```python
import jax
import jax.numpy as jnp
from jax import lax
from jax.sharding import PartitionSpec as P

NAMES = ("w_gate", "w_up", "w_down")


def matmul(a, w):
    return jnp.dot(a, w, preferred_element_type=jnp.float32).astype(jnp.bfloat16)


def normed(h):
    wide = h.astype(jnp.float32)
    scale = lax.rsqrt(jnp.mean(wide**2, -1, keepdims=True) + 1e-6)
    return (wide * scale).astype(jnp.bfloat16)


def layer(h, w):
    a = normed(h)
    gate = jnp.dot(a, w["w_gate"], preferred_element_type=jnp.float32)
    up = jnp.dot(a, w["w_up"], preferred_element_type=jnp.float32)
    return h + matmul((jax.nn.silu(gate) * up).astype(jnp.bfloat16), w["w_down"])


def adamw(w, m, v, g):
    m = 0.9 * m + 0.1 * g
    v = 0.95 * v + 0.05 * g * g
    step = m * lax.rsqrt(v + 1e-8) + 0.1 * w
    return (w - 0.02 * step).astype(jnp.bfloat16), m, v


def clipped(gradients, sum_of_squares, count):
    factor = jnp.minimum(1.0, 0.5 * lax.rsqrt(sum_of_squares / count + 1e-30))
    return [g * factor for g in gradients]


def solution(mesh):
    def fetched(weights, number):
        return {name: lax.all_gather(w[number], "dp", axis=0, tiled=True) for name, w in zip(NAMES, weights, strict=True)}

    def step(x, dy, *arrays):
        weights, m, v = (arrays[i : i + 3] for i in (0, 3, 6))
        layers = weights[0].shape[0]
        h, kept = x[0], []
        for number in range(layers):
            kept.append(h)
            h = layer(h, fetched(weights, number))
        by_h, mine = dy[0], [None] * layers
        for number in reversed(range(layers)):
            _, back = jax.vjp(lambda w, h: layer(h, w), fetched(weights, number), kept[number])
            by_w, by_h = back(by_h)
            mine[number] = [lax.psum_scatter(by_w[name], "dp", scatter_dimension=0, tiled=True) for name in NAMES]
        gradients = [jnp.stack([mine[number][i] for number in range(layers)]).astype(jnp.float32) for i in range(3)]
        squares = lax.psum(sum(jnp.sum(g * g) for g in gradients), "dp")
        gradients = clipped(gradients, squares, lax.psum(1, "dp") * sum(g.size for g in gradients))
        new = [adamw(w.astype(jnp.float32), m, v, g) for w, m, v, g in zip(weights, m, v, gradients, strict=True)]
        return tuple(one[which] for which in range(3) for one in new)

    states, cut = P(("rep", "dp"), None, None), P(None, "dp", None)
    return jax.shard_map(
        step,
        mesh=mesh,
        in_specs=(states, states) + (cut,) * 9,
        out_specs=(P("rep", "dp", None),) * 9,
        check_vma=False,
    )
```

profile of v0, /device:TPU:113, one launch (start us, length us, event | category | flops | bytes accessed | tf_op | source)
XLA Modules:
  0.0 539.4 jit_solution(15752536866008141536)
XLA Ops:
  7.3 2.4 fusion.94
  9.7 0.1 all-gather.15.cloned.1.call-start
  9.8 2.3 fusion.93
  12.2 0.1 all-gather.17.cloned.1.call-start
  12.2 1.1 fusion.92
  13.5 0.6 all-gather.23.cloned.1.call-update
  14.1 0.6 all-gather.21.cloned.1.call-update
  14.8 0.6 all-gather.19.cloned.1.call-update
  15.4 6.2 %copy.20 = bf16[1,2048,896]{1,2,0:T(8,128)(2,1)} copy(bf16[1,2048,896]{2,1,0:T(8,128)(2,1)} %param.11) | data formatting | bytes 7340032 | tf_op args[0]
  21.5 2.8 fusion.15
  24.4 6.2 %copy.21 = bf16[1,2048,896]{1,2,0:T(8,128)(2,1)} copy(bf16[1,2048,896]{2,1,0:T(8,128)(2,1)} %param.12) | data formatting | bytes 7340032 | tf_op args[1]
  30.5 12.2 %all-gather.13.cloned.1.call-done = bf16[1,896,2560]{2,1,0:T(8,128)(2,1)} async-done(((bf16[1,112,2560]{2,1,0:T(8,128)(2,1)}), bf16[1,896,2560]{2,1,0:T(8,128)(2,1)}) %all-gather.13.cloned.1.call-update) | async-done | bytes 4587536 | tf_op jit(solution)/shard_map/all_gather | solution.py:40
  42.8 18.1 %fusion.41 = f32[2048,2560]{1,0:T(8,128)} fusion(bf16[1,896,2560]{2,1,0:T(8,128)(2,1)} %all-gather.13.cloned.1.call-done, bf16[1,2048,896]{1,2,0:T(8,128)(2,1)} %copy.20, f32[2048]{0:T(1024)S(1)} %add_rsqrt_fusion), kind=kOutput, calls=%fused_computation.59 | convolution fusion | flops 9400745984 | bytes 29237248 | tf_op jit(solution)/shard_map/dot_general | solution.py:21
  60.9 13.4 %all-gather.15.cloned.1.call-done = bf16[1,896,2560]{2,1,0:T(8,128)(2,1)} async-done(((bf16[1,112,2560]{2,1,0:T(8,128)(2,1)}), bf16[1,896,2560]{2,1,0:T(8,128)(2,1)}) %all-gather.15.cloned.1.call-update) | async-done | bytes 4587536 | tf_op jit(solution)/shard_map/all_gather | solution.py:40
  74.3 28.0 %multiply_convert_fusion.1 = (bf16[2048,2560]{1,0:T(8,128)(2,1)}, f32[2048,2560]{1,0:T(8,128)}) fusion(f32[2048,2560]{1,0:T(8,128)} %fusion.41, bf16[1,896,2560]{2,1,0:T(8,128)(2,1)} %all-gather.15.cloned.1.call-done, bf16[1,2048,896]{1,2,0:T(8,128)(2,1)} %copy.20, f32[2048]{0:T(1024)S(1)} %add_rsqrt_fusion), kind=kOutput, calls=%fused_computation.17 | convolution fusion | flops 9432203264 | bytes 60694528 | tf_op jit(solution)/shard_map/dot_general | solution.py:22
  102.4 3.5 all-gather.17.cloned.1.call-done
  105.9 16.2 %fusion.19 = (f32[2048]{0:T(1024)S(1)}, bf16[2048,896]{0,1:T(8,128)(2,1)}) fusion(bf16[2048,2560]{1,0:T(8,128)(2,1)} %get-tuple-element.24, bf16[1,2560,896]{2,1,0:T(8,128)(2,1)} %all-gather.17.cloned.1.call-done, bf16[1,2048,896]{1,2,0:T(8,128)(2,1)} %copy.20), kind=kOutput, calls=%fused_computation.37 | convolution fusion | flops 9404413952 | bytes 22421504 | tf_op jit(solution)/shard_map/dot_general | solution.py:10
  122.1 15.2 %all-gather.23.cloned.1.call-done = bf16[1,896,2560]{2,1,0:T(8,128)(2,1)} async-done(((bf16[1,112,2560]{2,1,0:T(8,128)(2,1)}), bf16[1,896,2560]{2,1,0:T(8,128)(2,1)}) %all-gather.23.cloned.1.call-update) | async-done | bytes 4587536 | tf_op jit(solution)/shard_map/all_gather | solution.py:40
  137.3 18.4 %fusion.28 = f32[2048,2560]{1,0:T(8,128)} fusion(bf16[1,896,2560]{2,1,0:T(8,128)(2,1)} %all-gather.23.cloned.1.call-done, bf16[2048,896]{0,1:T(8,128)(2,1)} %get-tuple-element.27, f32[2048]{0:T(1024)S(1)} %fusion.80), kind=kOutput, calls=%fused_computation.46 | convolution fusion | flops 9400745984 | bytes 29237248 | tf_op jit(solution)/shard_map/jvp()/dot_general | solution.py:22
  155.7 12.9 %all-gather.21.cloned.1.call-done = bf16[1,2560,896]{2,1,0:T(8,128)(2,1)} async-done(((bf16[1,320,896]{2,1,0:T(8,128)(2,1)}), bf16[1,2560,896]{2,1,0:T(8,128)(2,1)}) %all-gather.21.cloned.1.call-update) | async-done | bytes 4587536 | tf_op jit(solution)/shard_map/all_gather | solution.py:40
  168.6 16.4 %convolution_convert_fusion.1 = bf16[2048,2560]{1,0:T(8,128)(2,1)} fusion(bf16[1,2560,896]{2,1,0:T(8,128)(2,1)} %all-gather.21.cloned.1.call-done, bf16[1,2048,896]{2,1,0:T(8,128)(2,1)} %param.12), kind=kOutput, calls=%fused_computation.27 | convolution fusion | flops 9400483840 | bytes 18743296 | tf_op jit(solution)/shard_map/transpose(jvp())/dot_general | solution.py:10
  185.0 15.0 %all-gather.19.cloned.1.call-done = bf16[1,896,2560]{2,1,0:T(8,128)(2,1)} async-done(((bf16[1,112,2560]{2,1,0:T(8,128)(2,1)}), bf16[1,896,2560]{2,1,0:T(8,128)(2,1)}) %all-gather.19.cloned.1.call-update) | async-done | bytes 4587536 | tf_op jit(solution)/shard_map/all_gather | solution.py:40
  200.0 31.7 %fusion.2 = (bf16[2048,2560]{1,0:T(8,128)(2,1)}, f32[2048,2560]{1,0:T(8,128)}) fusion(f32[2048,2560]{1,0:T(8,128)} %fusion.28, bf16[2048,2560]{1,0:T(8,128)(2,1)} %convolution_convert_fusion.1, bf16[1,896,2560]{2,1,0:T(8,128)(2,1)} %all-gather.19.cloned.1.call-done, bf16[2048,896]{0,1:T(8,128)(2,1)} %get-tuple-element.27, f32[2048]{0:T(1024)S(1)} %fusion.80), kind=kOutput, calls=%fused_computation.8 | convolution fusion | flops 9463660544 | bytes 71180288 | tf_op jit(solution)/shard_map/jvp()/dot_general | solution.py:21
  231.7 18.3 %fusion.12 = bf16[2048,896]{0,1:T(8,128)(2,1)} fusion(bf16[2048,2560]{1,0:T(8,128)(2,1)} %convolution_convert_fusion.1, bf16[1,896,2560]{2,1,0:T(8,128)(2,1)} %all-gather.23.cloned.1.call-done, f32[2048,2560]{1,0:T(8,128)} %get-tuple-element.29), kind=kOutput, calls=%fused_computation.21 | convolution fusion | flops 9426698240 | bytes 39714816 | tf_op jit(solution)/shard_map/transpose(jvp())/dot_general | solution.py:22
  250.0 15.3 %fusion.21 = (f32[2048]{0:T(1024)S(1)}, bf16[2048,896]{0,1:T(8,128)(2,1)S(1)}) fusion(bf16[2048,896]{0,1:T(8,128)(2,1)S(1)} %copy-done.5, bf16[2048,896]{0,1:T(8,128)(2,1)} %fusion.12, bf16[2048,2560]{1,0:T(8,128)(2,1)} %get-tuple-element.28, bf16[1,896,2560]{2,1,0:T(8,128)(2,1)} %all-gather.19.cloned.1.call-done), kind=kOutput, calls=%fused_computation.39 | convolution fusion | flops 9404413952 | bytes 26091520 | tf_op jit(solution)/shard_map/transpose(jvp())/dot_general | solution.py:21
  265.4 2.7 fusion.43
  268.1 1.8 copy-done.6
  269.9 15.3 %convolution_convert_fusion.2 = bf16[2560,896]{1,0:T(8,128)(2,1)} fusion(bf16[2048,2560]{1,0:T(8,128)(2,1)} %get-tuple-element.24, bf16[2048,896]{0,1:T(8,128)(2,1)S(1)} %fusion.43), kind=kOutput, calls=%fused_computation.44 | convolution fusion | flops 9397534720 | bytes 18743296 | tf_op jit(solution)/shard_map/transpose(jvp())/dot_general | solution.py:10
  285.3 0.1 reduce-scatter.17.cloned.1.call-start
  285.3 21.5 %fusion.27 = bf16[2560,896]{1,0:T(8,128)(2,1)} fusion(f32[2048,2560]{1,0:T(8,128)} %fusion.28, bf16[1,2048,896]{2,1,0:T(8,128)(2,1)} %param.12, f32[2048,2560]{1,0:T(8,128)} %get-tuple-element.29), kind=kOutput, calls=%fused_computation.43 | convolution fusion | flops 9428992000 | bytes 50200576 | tf_op jit(solution)/shard_map/transpose(jvp())/dot_general | solution.py:10
  307.0 16.5 %convolution_convert_fusion = bf16[2048,2560]{1,0:T(8,128)(2,1)} fusion(bf16[2048,896]{0,1:T(8,128)(2,1)} %copy-done.6, bf16[1,2560,896]{2,1,0:T(8,128)(2,1)} %all-gather.17.cloned.1.call-done), kind=kOutput, calls=%fused_computation.26 | convolution fusion | flops 9400483840 | bytes 18743296 | tf_op jit(solution)/shard_map/transpose(jvp())/dot_general | solution.py:10
  323.5 18.6 %fusion.26 = bf16[896,2560]{1,0:T(8,128)(2,1)} fusion(bf16[2048,2560]{1,0:T(8,128)(2,1)} %convolution_convert_fusion, f32[2048,2560]{1,0:T(8,128)} %fusion.41, bf16[1,2048,896]{1,2,0:T(8,128)(2,1)} %copy.20, f32[2048]{0:T(1024)S(1)} %copy-done.15), kind=kOutput, calls=%fused_computation.42 | convolution fusion | flops 9434497024 | bytes 39723008 | tf_op jit(solution)/shard_map/transpose(jvp())/dot_general | solution.py:22
  342.2 0.1 reduce-scatter.13.cloned.1.call-start
  342.3 18.8 %fusion.25 = bf16[896,2560]{1,0:T(8,128)(2,1)} fusion(bf16[2048,2560]{1,0:T(8,128)(2,1)} %convolution_convert_fusion.1, bf16[2048,896]{0,1:T(8,128)(2,1)} %get-tuple-element.27, f32[2048]{0:T(1024)S(1)} %fusion.80, f32[2048,2560]{1,0:T(8,128)} %get-tuple-element.29), kind=kOutput, calls=%fused_computation.41 | convolution fusion | flops 9434497024 | bytes 39723008 | tf_op jit(solution)/shard_map/transpose(jvp())/dot_general | solution.py:22
  361.2 24.2 %fusion.22 = bf16[896,2560]{1,0:T(8,128)(2,1)} fusion(f32[2048,2560]{1,0:T(8,128)} %fusion.41, f32[2048,2560]{1,0:T(8,128)} %get-tuple-element.25, bf16[2048,2560]{1,0:T(8,128)(2,1)} %convolution_convert_fusion, bf16[1,2048,896]{1,2,0:T(8,128)(2,1)} %copy.20, f32[2048]{0:T(1024)S(1)} %copy-done.15), kind=kOutput, calls=%fused_computation.40 | convolution fusion | flops 9460711424 | bytes 60694528 | tf_op jit(solution)/shard_map/transpose(jvp())/dot_general | solution.py:21
  385.6 15.1 %convolution_convert_fusion.3 = bf16[896,2560]{1,0:T(8,128)(2,1)} fusion(bf16[2048,2560]{1,0:T(8,128)(2,1)} %get-tuple-element.28, bf16[2048,896]{0,1:T(8,128)(2,1)} %get-tuple-element.27, f32[2048]{0:T(1024)S(1)} %fusion.80), kind=kOutput, calls=%fused_computation.45 | convolution fusion | flops 9400745984 | bytes 18751488 | tf_op jit(solution)/shard_map/transpose(jvp())/dot_general | solution.py:21
  400.8 2.6 fusion.70
  403.4 21.6 %reduce-scatter.13.cloned.1.call-done = bf16[112,2560]{1,0:T(8,128)(2,1)} async-done(((bf16[896,2560]{1,0:T(8,128)(2,1)}), bf16[112,2560]{1,0:T(8,128)(2,1)}) %reduce-scatter.13.cloned.1.call-update) | async-done | bytes 573456 | tf_op jit(solution)/shard_map/reduce_scatter | solution.py:53
  425.1 2.4 fusion.69
  427.5 33.6 %reduce-scatter.7.cloned.1.call-done = bf16[112,2560]{1,0:T(8,128)(2,1)} async-done(((bf16[896,2560]{1,0:T(8,128)(2,1)}), bf16[112,2560]{1,0:T(8,128)(2,1)}) %reduce-scatter.7.cloned.1.call-update) | async-done | bytes 573456 | tf_op jit(solution)/shard_map/reduce_scatter | solution.py:53
  461.1 35.9 %reduce-scatter.9.cloned.1.call-done = bf16[112,2560]{1,0:T(8,128)(2,1)} async-done(((bf16[896,2560]{1,0:T(8,128)(2,1)}), bf16[112,2560]{1,0:T(8,128)(2,1)}) %reduce-scatter.9.cloned.1.call-update) | async-done | bytes 573456 | tf_op jit(solution)/shard_map/reduce_scatter | solution.py:53
  497.0 2.4 fusion.68
  501.4 15.8 %psum.7 = f32[]{:T(128)} all-reduce(f32[]{:T(128)S(6)} %add.99), channel_id=1, replica_groups=mesh['rep'=2,'dp'=8] {'dp'}, use_global_device_ids=true, to_apply=%region_12.13 | all-reduce | flops 1 | bytes 8 | tf_op jit(solution)/shard_map/psum | solution.py:55
  518.0 5.5 %fusion.76 = (bf16[2,320,896]{2,1,0:T(8,128)(2,1)}, f32[2,320,896]{2,1,0:T(8,128)}, f32[2,320,896]{2,1,0:T(8,128)}) fusion(bf16[2,320,896]{2,1,0:T(8,128)(2,1)S(1)} %copy-done.2, f32[]{:T(128)S(6)} %min_shard_map.3, bf16[1,320,896]{2,1,0:T(8,128)(2,1)} %bitcast.69, bf16[1,320,896]{2,1,0:T(8,128)(2,1)} %bitcast.67, f32[2,320,896]{2,1,0:T(8,128)S(1)} %copy-done.7, ...), kind=kLoop, calls=%fused_computation.98 | loop fusion | flops 11468800 | bytes 12615684 | tf_op jit(solution)/shard_map/convert_element_type | solution.py:30
  523.5 1.2 copy-done.10
  524.7 0.7 copy-done.11
  525.4 0.2 copy-done.13
  525.5 6.6 %fusion.67 = (bf16[2,112,2560]{2,1,0:T(8,128)(2,1)}, f32[2,112,2560]{2,1,0:T(8,128)}, f32[2,112,2560]{2,1,0:T(8,128)}, bf16[2,112,2560]{2,1,0:T(8,128)(2,1)}, f3...) fusion(bf16[2,112,2560]{2,1,0:T(8,128)(2,1)S(1)} %copy-done.3, f32[]{:T(128)S(6)} %min_shard_map.3, ...), kind=kLoop, calls=%fused_computation.89 | loop fusion | flops 22937600 | bytes 25231364 | tf_op jit(solution)/shard_map/convert_element_type | solution.py:30
  (51 shorter events, 1.2 us)
Async XLA Ops:
  7.2 5.0 copy-start.1
  7.2 35.6 %all-gather.13.cloned.1.call-start = ((), (), s32[]{:S(2)}) async-start(), calls=%async_computation.12 | async-start | bytes 5160960 | tf_op jit(solution)/shard_map/all_gather | solution.py:40
  9.7 64.6 %all-gather.15.cloned.1.call-start = ((), (), s32[]{:S(2)}) async-start(), calls=%async_computation.13 | async-start | bytes 5160960 | tf_op jit(solution)/shard_map/all_gather | solution.py:40
  12.2 93.7 %all-gather.17.cloned.1.call-start = ((), (), s32[]{:S(2)}) async-start(), calls=%async_computation.14 | async-start | bytes 5160960 | tf_op jit(solution)/shard_map/all_gather | solution.py:40
  13.4 123.9 %all-gather.23.cloned.1.call-start = ((), (), s32[]{:S(2)}) async-start(), calls=%async_computation.17 | async-start | bytes 5160960 | tf_op jit(solution)/shard_map/all_gather | solution.py:40
  14.0 154.6 %all-gather.21.cloned.1.call-start = ((), (), s32[]{:S(2)}) async-start(), calls=%async_computation.16 | async-start | bytes 5160960 | tf_op jit(solution)/shard_map/all_gather | solution.py:40
  14.7 185.3 %all-gather.19.cloned.1.call-start = ((), (), s32[]{:S(2)}) async-start(), calls=%async_computation.15 | async-start | bytes 5160960 | tf_op jit(solution)/shard_map/all_gather | solution.py:40
  15.3 385.5 %reduce-scatter.15.cloned.1.call-start = ((), (), s32[]{:S(2)}) async-start(), calls=%async_computation.10 | async-start | bytes 5160960 | tf_op jit(solution)/shard_map/reduce_scatter | solution.py:53
  24.4 50.0 %copy-start.14 = (f32[2048]{0:T(1024)}, f32[2048]{0:T(1024)S(1)}, u32[]{:S(2)}) copy-start(f32[2048]{0:T(1024)S(1)} %add_rsqrt_fusion) | copy-start | bytes 24580
  231.7 18.3 %copy-start.5 = (bf16[2048,896]{0,1:T(8,128)(2,1)S(1)}, bf16[2048,896]{0,1:T(8,128)(2,1)}, u32[]{:S(2)}) copy-start(bf16[2048,896]{0,1:T(8,128)(2,1)} %get-tuple-element.27) | copy-start | bytes 11010052
  250.0 15.3 %copy-start = (bf16[1,2048,896]{1,2,0:T(8,128)(2,1)S(1)}, bf16[1,2048,896]{1,2,0:T(8,128)(2,1)}, u32[]{:S(2)}) copy-start(bf16[1,2048,896]{1,2,0:T(8,128)(2,1)} %copy.21) | copy-start | bytes 11010052
  268.1 1.8 copy-start.6
  285.3 115.6 %reduce-scatter.17.cloned.1.call-start = ((), (), s32[]{:S(2)}) async-start(), calls=%async_computation.11 | async-start | bytes 5160960 | tf_op jit(solution)/shard_map/reduce_scatter | solution.py:53
  306.9 16.6 %copy-start.15 = (f32[2048]{0:T(1024)S(1)}, f32[2048]{0:T(1024)}, u32[]{:S(2)}) copy-start(f32[2048]{0:T(1024)} %copy-done.14) | copy-start | bytes 24580
  306.9 96.5 %reduce-scatter.11.cloned.1.call-start = ((), (), s32[]{:S(2)}) async-start(), calls=%async_computation.8 | async-start | bytes 5160960 | tf_op jit(solution)/shard_map/reduce_scatter | solution.py:53
  342.2 82.9 %reduce-scatter.13.cloned.1.call-start = ((), (), s32[]{:S(2)}) async-start(), calls=%async_computation.9 | async-start | bytes 5160960 | tf_op jit(solution)/shard_map/reduce_scatter | solution.py:53
  361.1 100.0 %reduce-scatter.7.cloned.1.call-start = ((), (), s32[]{:S(2)}) async-start(), calls=%async_computation.6 | async-start | bytes 5160960 | tf_op jit(solution)/shard_map/reduce_scatter | solution.py:53
  385.5 111.5 %reduce-scatter.9.cloned.1.call-start = ((), (), s32[]{:S(2)}) async-start(), calls=%async_computation.7 | async-start | bytes 5160960 | tf_op jit(solution)/shard_map/reduce_scatter | solution.py:53
  400.7 117.1 %copy-start.2 = (bf16[2,320,896]{2,1,0:T(8,128)(2,1)S(1)}, bf16[2,320,896]{2,1,0:T(8,128)(2,1)}, u32[]{:S(2)}) copy-start(bf16[2,320,896]{2,1,0:T(8,128)(2,1)} %param.15) | copy-start | bytes 3440644
  400.7 117.2 %copy-start.7 = (f32[2,320,896]{2,1,0:T(8,128)S(1)}, f32[2,320,896]{2,1,0:T(8,128)}, u32[]{:S(2)}) copy-start(f32[2,320,896]{2,1,0:T(8,128)} %param.21) | copy-start | bytes 6881284
  517.9 5.6 %copy-start.3 = (bf16[2,112,2560]{2,1,0:T(8,128)(2,1)S(1)}, bf16[2,112,2560]{2,1,0:T(8,128)(2,1)}, u32[]{:S(2)}) copy-start(bf16[2,112,2560]{2,1,0:T(8,128)(2,1)} %param.13) | copy-start | bytes 3440644
  517.9 5.6 %copy-start.4 = (bf16[2,112,2560]{2,1,0:T(8,128)(2,1)S(1)}, bf16[2,112,2560]{2,1,0:T(8,128)(2,1)}, u32[]{:S(2)}) copy-start(bf16[2,112,2560]{2,1,0:T(8,128)(2,1)} %param.14) | copy-start | bytes 3440644
  517.9 5.6 %copy-start.8 = (f32[2,112,2560]{2,1,0:T(8,128)S(1)}, f32[2,112,2560]{2,1,0:T(8,128)}, u32[]{:S(2)}) copy-start(f32[2,112,2560]{2,1,0:T(8,128)} %param.19) | copy-start | bytes 6881284
  517.9 5.6 %copy-start.9 = (f32[2,112,2560]{2,1,0:T(8,128)S(1)}, f32[2,112,2560]{2,1,0:T(8,128)}, u32[]{:S(2)}) copy-start(f32[2,112,2560]{2,1,0:T(8,128)} %param.16) | copy-start | bytes 6881284
  517.9 6.7 %copy-start.10 = (f32[2,112,2560]{2,1,0:T(8,128)S(1)}, f32[2,112,2560]{2,1,0:T(8,128)}, u32[]{:S(2)}) copy-start(f32[2,112,2560]{2,1,0:T(8,128)} %param.20) | copy-start | bytes 6881284
  517.9 7.4 %copy-start.11 = (f32[2,112,2560]{2,1,0:T(8,128)S(1)}, f32[2,112,2560]{2,1,0:T(8,128)}, u32[]{:S(2)}) copy-start(f32[2,112,2560]{2,1,0:T(8,128)} %param.17) | copy-start | bytes 6881284
  518.0 7.4 %copy-start.12 = (bf16[112,2560]{1,0:T(8,128)(2,1)S(1)}, bf16[112,2560]{1,0:T(8,128)(2,1)}, u32[]{:S(2)}) copy-start(bf16[112,2560]{1,0:T(8,128)(2,1)} %reduce-scatter.11.cloned.1.call-done) | copy-start | bytes 1720324
  518.0 7.6 %copy-start.13 = (bf16[112,2560]{1,0:T(8,128)(2,1)S(1)}, bf16[112,2560]{1,0:T(8,128)(2,1)}, u32[]{:S(2)}) copy-start(bf16[112,2560]{1,0:T(8,128)(2,1)} %reduce-scatter.13.cloned.1.call-done) | copy-start | bytes 1720324
Sparse Core Ops, SparseCore 0:
  10.2 32.5 all-gather.12
  44.9 29.3 all-gather.14
  76.5 29.3 all-gather.16
  107.9 29.3 all-gather.22
  139.3 29.3 all-gather.20
  170.6 29.3 all-gather.18
  285.4 31.5 reduce-scatter.14
  319.3 33.7 reduce-scatter.16
  355.4 33.6 reduce-scatter.10
  391.3 33.6 reduce-scatter.12
  427.4 33.6 reduce-scatter.6
  463.3 33.6 reduce-scatter.8
where the time goes:
time: 547 us; the launch traced here: 539 us
  matrix products  293 us (54%)
  waiting for transfers between devices  166 us (30%)
  other arithmetic  25 us (5%)
  local copies, waits for them, and re-layouts  22 us (4%)
  between operations  17.5 us (3%)
  blocking collectives  15.8 us (3%)
    dot_general x5, matrix products, layer(): gate = jnp.dot(a, w['w_gate'], preferred_element_type=jnp.float32)  104 us
    dot_general x5, matrix products, layer(): up = jnp.dot(a, w['w_up'], preferred_element_type=jnp.float32)  102 us
    reduce_scatter x6, waiting for transfers between devices, step(): lax.psum_scatter(by_w[name], 'dp', scatter_dimension=0, tiled=True)  91.2 us
    dot_general x5, matrix products, matmul(): jnp.dot(a, w, preferred_element_type=jnp.float32).astype(jnp.bfloat16)  85.9 us
    all_gather x6, waiting for transfers between devices, fetched(): lax.all_gather(w[number], 'dp', axis=0, tiled=True)  72.3 us
    unnamed x34, local copies, waits for them, and re-layouts  16.2 us
    psum x1, blocking collectives, step(): squares = lax.psum(sum((jnp.sum(g * g) for g in gradients)), 'dp')  15.8 us
    convert_element_type x2, other arithmetic, adamw(): return ((w - 0.02 * step).astype(jnp.bfloat16), m, v)  12.1 us
  transfers between devices with their start and end apart: 12, of which 9 were waited for; matrix products, arithmetic and copies ran while one was open for 44% of the time, Pallas kernels for 0%

commit v1 on v0

v1 whole, which is shorter than its diff:
```python
import functools

import jax
import jax.numpy as jnp
from jax import lax
from jax.experimental import pallas as pl
from jax.experimental.pallas import tpu as pltpu
from jax.sharding import PartitionSpec as P

MESH = pl.DeviceIdType.MESH
BF, F32 = jnp.bfloat16, jnp.float32
CH = 512
SUB = 256
VMEM_LIMIT = 67_043_328
FIRST, SECOND, ALL = 0, 1, None


def dot(a, b, ca, cb):
    return lax.dot_general(a, b, (((ca,), (cb,)), ((), ())), preferred_element_type=F32)


nn = functools.partial(dot, ca=1, cb=0)
nt = functools.partial(dot, ca=1, cb=1)
tn = functools.partial(dot, ca=0, cb=0)


def place():
    me = lax.axis_index("dp")
    x, k = me // 2, me % 2
    chips = (x, x + 1 - 2 * (x % 2), (x + 2) % 4, 3 - x)
    return me, k, chips, [2 * c + k for c in chips], [2 * c + 1 - k for c in chips]


def meet(devices):
    barrier = pltpu.get_barrier_semaphore()
    for d in devices:
        pl.semaphore_signal(barrier, device_id={"dp": d}, device_id_type=MESH)
    pl.semaphore_wait(barrier, len(devices))


def remote(src, dst, send, recv, device):
    return pltpu.make_async_remote_copy(src_ref=src, dst_ref=dst, send_sem=send, recv_sem=recv, device_id={"dp": device}, device_id_type=MESH)


def when(condition, *acts):
    @pl.when(condition)
    def _():
        for act in acts:
            act()


def tile(t, size):
    return pl.ds(pl.multiple_of(t * size, size), size)


def lanes(start, size):
    return pl.ds(start if isinstance(start, int) else pl.multiple_of(start, 128), size)


class Local:
    def __init__(self, sems):
        self.sems, self.used = sems, 0

    def __call__(self, src, dst):
        copy = pltpu.make_async_copy(src, dst, self.sems.at[self.used])
        self.used += 1
        copy.start()
        return copy


def normed(h):
    wide = h.astype(F32)
    scale = lax.rsqrt(jnp.mean(wide * wide, -1, keepdims=True) + 1e-6)
    return (wide * scale).astype(BF)


def norm_rows(src, dst):
    @pl.loop(0, src.shape[0] // SUB)
    def _(t):
        dst[tile(t, SUB), :] = normed(src[tile(t, SUB), :])


def squares(g):
    g = g.astype(F32)
    return jnp.sum((g * g).reshape(-1, 8, g.shape[-1]), 0)


class Gather:
    def __init__(self, send, recv):
        self.send, self.recv = send, recv
        self.me, k, chips, (n0, n1, n2, n3), (o0, o1, o2, o3) = place()
        self.partners = (n1, n3, o0)
        self.moves = [
            (n0, ALL, n1), (n0, ALL, n3), (n0, ALL, o0), (n1, FIRST, n3), (n3, SECOND, n1),
            (n1, ALL, o0), (n3, ALL, o0), (n2, FIRST, o0), (n2, SECOND, o0),
        ]
        self.lands = [(n1, ALL), (n3, ALL), (o0, ALL), (n2, FIRST), (n2, SECOND), (o1, ALL), (o3, ALL), (o2, FIRST), (o2, SECOND)]

    def region(self, item, dev, half):
        src, layer, at, buf, blk, r0, rn, c0, cn, by_rows = item
        row = dev * blk + r0
        if half is not ALL:
            if by_rows:
                rn //= 2
                row = row + half * rn
            else:
                cn //= 2
                c0 = c0 + half * cn
        return buf.at[pl.ds(pl.multiple_of(row, 16), rn), lanes(c0, cn)]

    def nth(self, i, item, c):
        source, half, to = self.moves[c]
        src = dst = self.region(item, source, half)
        if source is self.moves[0][0]:
            array, layer, at, buf, blk, r0, rn, c0, cn, by_rows = item
            src = array.at[layer, pl.ds(r0, rn), lanes(at, cn)]
        return remote(src, dst, self.send.at[i, c], self.recv.at[i, c], to)

    def arrived(self, i, item, c):
        what = self.region(item, *self.lands[c])
        remote(what, what, self.send.at[i, c], self.recv.at[i, c], self.partners[0]).wait_recv()

    def issue(self, piece):
        for i, item in piece:
            for c in (0, 1, 2):
                self.nth(i, item, c).start()

    def forward(self, piece):
        for i, item in piece:
            for c in (0, 1):
                self.arrived(i, item, c)
                self.nth(i, item, c + 3).start()
                self.nth(i, item, c + 5).start()

    def pass_on(self, piece):
        for i, item in piece:
            for c in (3, 4):
                self.arrived(i, item, c)
                self.nth(i, item, c + 4).start()

    def complete(self, piece):
        for i, item in piece:
            for c in (2, 5, 6, 7, 8):
                self.arrived(i, item, c)

    def sent(self, piece):
        for i, item in piece:
            for c in range(len(self.moves)):
                self.nth(i, item, c).wait_send()


def pair(layer, r, weights, W, f):
    return [(2 * f + m, (w, layer, f * CH, W, r, 0, r, (2 * f + m) * CH, CH, False)) for m, w in enumerate(weights)]


def own_rows(keep, layer, r, weights, W, me):
    nf = W.shape[1] // (2 * CH)
    return [keep(w.at[layer, :, pl.ds(f * CH, CH)], W.at[tile(me, r), pl.ds((2 * f + m) * CH, CH)]) for m, w in enumerate(weights) for f in range(nf)]


def forward_kernel(x_ref, wg_ref, wu_ref, wd_ref, h1_ref, a0_ref, g0_ref, u0_ref, wd0_ref, wd1_ref,
                   X, A, ACT, W, WD, GS, US, local, save, send, recv):
    T, D = X.shape
    F = ACT.shape[1]
    TM = GS.shape[1]
    r, rd, nf, tiles = wg_ref.shape[1], wd_ref.shape[1], F // CH, T // TM
    g, keep = Gather(send, recv), Local(local)
    x_in = keep(x_ref, X)
    own = own_rows(keep, 0, r, (wg_ref, wu_ref), W, g.me)
    own += [keep(wd_ref.at[layer], to.at[tile(g.me, rd), :]) for layer, to in enumerate((WD, wd1_ref))]
    meet(g.partners)
    chunk = functools.partial(pair, 0, r, (wg_ref, wu_ref), W)
    rest = [
        [(2 * (nf + layer) + i, (wd_ref, layer, 0, buf, rd, i * (rd // 2), rd // 2, 0, D, True))]
        for layer, buf in enumerate((WD, wd1_ref)) for i in range(2)
    ]

    def on(act, p, condition=True):
        when(condition & (p < nf), lambda: act(chunk(p)))
        for i, piece in enumerate(rest):
            when(condition & (p == nf + i), lambda: act(piece))

    ahead = 2
    for p in range(ahead):
        g.issue(chunk(p))
    x_in.wait()
    norm_rows(X, A)
    out = [keep(A, a0_ref), own.pop()]
    for c in own:
        c.wait()
    for p in range(ahead):
        g.forward(chunk(p))
        g.issue(chunk(p + ahead))
    g.pass_on(chunk(0))

    def saving(f, t):
        rows, cols, slot = tile(t, TM), tile(f, CH), t % 2
        return [pltpu.make_async_copy(S.at[slot], ref.at[rows, cols], save.at[i, slot]) for i, (S, ref) in enumerate(((GS, g0_ref), (US, u0_ref)))]

    @pl.loop(0, nf)
    def _(f):
        g.complete(chunk(f))

        @pl.loop(0, tiles)
        def _(t):
            on(g.forward, f + 2, t == tiles // 2)
            on(g.issue, f + 4, t == tiles // 2)
            copies, slot = saving(f, t), t % 2
            when((t > 1) | (f > 0), *[c.wait for c in copies])
            for j in range(TM // SUB):
                rows, part = tile(t * (TM // SUB) + j, SUB), pl.ds(j * SUB, SUB)
                both = nn(A[rows, :], W[:, tile(f, 2 * CH)])
                gate, up = both[:, :CH], both[:, CH:]
                GS[slot, part, :] = gate
                US[slot, part, :] = up
                ACT[rows, tile(f, CH)] = (gate * jax.nn.sigmoid(gate) * up).astype(BF)
            for c in copies:
                c.start()

        on(g.pass_on, f + 1)

    first, below, *last = rest
    g.complete(first)
    g.forward(last[0])
    g.pass_on(below)
    g.complete(below)
    out.append(keep(WD, wd0_ref))

    @pl.loop(0, T // CH)
    def _(t):
        rows = tile(t, CH)
        X[rows, :] = (X[rows, :].astype(F32) + nn(ACT[rows, :], WD[...]).astype(BF).astype(F32)).astype(BF)
        when(t == 0, lambda: g.forward(last[1]))
        when(t == 1, lambda: g.pass_on(last[0]))
        when(t == 2, lambda: g.pass_on(last[1]))

    out.append(keep(X, h1_ref))
    for p in last:
        g.complete(p)
    for p in [chunk(f) for f in range(nf)] + rest:
        g.sent(p)
    for t in range(tiles - 2, tiles):
        out += saving(nf - 1, t)
    for c in out:
        c.wait()


class Scatter:
    def __init__(self, r, refs, G, SQ, outs, sems):
        self.outs, self.saves = outs, sems
        self.R, (self.DS, self.DR), (self.AS, self.AR), (self.BS, self.BR), (self.CS, self.CR), (self.ES, self.ER) = refs[0], *zip(refs[1:-1:2], refs[2:-1:2])
        self.r, self.sems, self.G, self.SQ = r, refs[-1], G, SQ
        self.me, self.k, self.chips, (n0, n1, n2, n3), (o0, *_) = place()
        self.routes = ((self.DS, self.DR, o0), (self.AS, self.AR, n1), (self.BS, self.BR, n3), (self.CS, self.CR, n3), (self.ES, self.ER, n1))

    @staticmethod
    def scratch(r):
        sent = [(4, r, 2 * CH), (2, r, CH), (2, r, CH), (r, CH), (r, CH)]
        shapes = [s for one in sent for s in (one, (2, *one))]
        return [pltpu.VMEM((2, 8 * r, 2 * CH), F32), *[pltpu.VMEM(s, BF) for s in shapes], pltpu.SemaphoreType.DMA((5, 3))]

    def cp(self, which, f):
        src, dst, dev = self.routes[which]
        return remote(src, dst.at[f % 2], self.sems.at[which, 0], self.sems.at[which, 1 + f % 2], dev)

    def rows(self, q, core):
        return pl.ds(pl.multiple_of((2 * self.chips[q] + core) * self.r, 16), self.r)

    def dot_and_send(self, f, a, b):
        R = self.R.at[f % 2]
        R[...] = tn(a, b)
        when(f > 0, self.cp(0, f).wait_send)
        for q in range(4):
            self.DS[q] = R[self.rows(q, 1 - self.k), :].astype(BF)
        self.cp(0, f).start()

    def halve(self, f):
        s, R = f % 2, self.R.at[f % 2]
        self.cp(0, f).wait_recv()
        when(f > 0, self.cp(1, f).wait_send, self.cp(2, f).wait_send)
        v = [R[self.rows(q, self.k), :] + self.DR[s, q].astype(F32) for q in range(4)]
        self.AS[0], self.AS[1] = v[1][:, :CH].astype(BF), v[2][:, :CH].astype(BF)
        self.BS[0], self.BS[1] = v[3][:, CH:].astype(BF), v[2][:, CH:].astype(BF)
        R[self.rows(0, self.k), :] = v[0]
        R[self.rows(1, self.k), CH:] = v[1][:, CH:]
        R[self.rows(3, self.k), :CH] = v[3][:, :CH]
        self.cp(1, f).start()
        self.cp(2, f).start()

    def quarter(self, f):
        s, R, mine = f % 2, self.R.at[f % 2], self.rows(0, self.k)
        for which in (1, 2):
            self.cp(which, f).wait_recv()
        when(f > 0, self.cp(3, f).wait_send, self.cp(4, f).wait_send)
        self.CS[...] = (R[self.rows(3, self.k), :CH] + self.AR[s, 1].astype(F32)).astype(BF)
        self.ES[...] = (R[self.rows(1, self.k), CH:] + self.BR[s, 1].astype(F32)).astype(BF)
        self.cp(3, f).start()
        self.cp(4, f).start()
        R[mine, :CH] += self.AR[s, 0].astype(F32)
        R[mine, CH:] += self.BR[s, 0].astype(F32)

    def finish(self, f):
        s = f % 2
        for which in (3, 4):
            self.cp(which, f).wait_recv()
        v = self.R[s, self.rows(0, self.k), :]
        for m, (part, last) in enumerate(((v[:, :CH], self.CR), (v[:, CH:], self.ER))):
            g = (part + last[s].astype(F32)).astype(BF)
            when(f > 1, self.saving(f, m).wait)
            self.G[s, m] = g
            self.saving(f, m).start()
            self.SQ[...] += squares(g)

    def saving(self, f, m):
        return pltpu.make_async_copy(self.G.at[f % 2, m], self.outs[m].at[:, tile(f, CH)], self.saves.at[m, f % 2])

    def drain(self, f):
        for which in range(len(self.routes)):
            self.cp(which, f).wait_send()
        for m in range(2):
            self.saving(f, m).wait()
            self.saving(f - 1, m).wait()


def swiglu_back(gate, up, dact):
    sig = jax.nn.sigmoid(gate)
    silu = gate * sig
    dact = dact.astype(F32)
    return (silu * up).astype(BF), (dact * up * (sig + silu * (1.0 - sig))).astype(BF), (dact * silu).astype(BF)


def last_kernel(h1_ref, dy_ref, wg_ref, wu_ref, wd1_ref, gg_ref, gu_ref, act1_ref, dh1_ref, sq_ref,
                A, DY, W, WD, DGU, ACT, G, SQ, local, save, gsem, send, recv, *scatter):
    T, D = A.shape
    F = W.shape[1] // 2
    TM = 4 * SUB
    r, nf, tiles = wg_ref.shape[1], F // CH, T // TM
    g, keep = Gather(send, recv), Local(local)
    s = Scatter(r, scatter, G, SQ, (gg_ref.at[1], gu_ref.at[1]), gsem)
    h_in, dy_in, wd_in = keep(h1_ref, A), keep(dy_ref, DY), keep(wd1_ref, WD)
    own = own_rows(keep, 1, r, (wg_ref, wu_ref), W, g.me)
    meet(g.partners)
    piece = functools.partial(pair, 1, r, (wg_ref, wu_ref), W)
    g.issue(piece(0))
    SQ[...] = jnp.zeros_like(SQ)
    h_in.wait()
    norm_rows(A, A)
    dy_in.wait()
    wd_in.wait()

    @pl.loop(0, T // CH)
    def _(t):
        rows = tile(t, CH)
        dact = nt(DY[rows, :], WD[...]).astype(BF)
        for f in range(nf):
            DGU[rows, pl.ds((2 * f + 1) * CH, CH)] = dact[:, f * CH : (f + 1) * CH]
        when(t == 0, lambda: g.forward(piece(0)), lambda: g.issue(piece(1)))
        when(t == 1, lambda: g.issue(piece(2)))
        when(t == 2, lambda: g.pass_on(piece(0)))

    for c in own:
        c.wait()

    def save_act(f):
        return pltpu.make_async_copy(ACT, act1_ref.at[:, tile(f, CH)], save.at[0])

    @pl.loop(0, nf)
    def _(f):
        cols = tile(f, 2 * CH)
        g.complete(piece(f))
        when(f > 0, lambda: save_act(f).wait())

        @pl.loop(0, tiles)
        def _(t):
            when((t == 0) & (f > 1), lambda: s.quarter(f - 2))
            when((t == 0) & (f + 1 < nf), lambda: g.forward(piece(f + 1)))
            when((t == 0) & (f + 3 < nf), lambda: g.issue(piece(f + 3)))
            when((t == 1) & (f > 0), lambda: s.halve(f - 1))
            for j in range(TM // SUB):
                rows = tile(t * (TM // SUB) + j, SUB)
                both = nn(A[rows, :], W[:, cols])
                ACT[rows, :], DGU[rows, tile(2 * f, CH)], DGU[rows, tile(2 * f + 1, CH)] = swiglu_back(both[:, :CH], both[:, CH:], DGU[rows, tile(2 * f + 1, CH)])

        save_act(f).start()
        when(f + 1 < nf, lambda: g.pass_on(piece(f + 1)))
        when(f > 1, lambda: s.finish(f - 2))
        s.dot_and_send(f, A[...], DGU[:, cols])

    save_act(nf - 1).wait()
    keep(h1_ref, A).wait()

    @pl.loop(0, T // CH)
    def _(t):
        rows = tile(t, CH)
        da = nt(DGU[rows, :], W[...]).astype(BF).astype(F32)
        wide = A[rows, :].astype(F32)
        scale = lax.rsqrt(jnp.mean(wide * wide, -1, keepdims=True) + 1e-6)
        back = (da * scale - wide * (scale * scale * scale * jnp.mean(da * wide, -1, keepdims=True))).astype(BF)
        DY[rows, :] = (DY[rows, :].astype(F32) + back.astype(F32)).astype(BF)
        when(t == 0, lambda: s.quarter(nf - 2), lambda: s.halve(nf - 1))
        when(t == 1, lambda: s.finish(nf - 2), lambda: s.quarter(nf - 1))
        when(t == 2, lambda: s.finish(nf - 1))

    out = [keep(DY, dh1_ref)]
    sq_ref[...] = jnp.full(sq_ref.shape, jnp.sum(SQ[...]), F32)
    for f in range(nf):
        g.sent(piece(f))
    s.drain(nf - 1)
    for c in out:
        c.wait()


class DownScatter:
    def __init__(self, rd, refs, GD, SQ):
        (self.PT, self.PD, self.DS, self.DR, self.S1, self.R1, self.S3, self.R3, self.Q1, self.Q3, self.sems) = refs
        self.rd, self.GD, self.SQ = rd, GD, SQ
        self.me, self.k, self.chips, (n0, n1, n2, n3), (self.partner, *_) = place()
        near = ((self.S1, self.R1, n1), (self.S3, self.R3, n3))
        self.routes = [(S.at[i], R.at[i], n) for S, R, n in near for i in range(2)] + [(self.S1.at[0], self.Q1, n1), (self.S3.at[0], self.Q3, n3)]
        h = rd // 2
        self.top, self.low = slice(0, h), slice(h, rd)

    @staticmethod
    def scratch(rd, D):
        V = pltpu.VMEM
        return [
            V((2 * rd, D), F32), V((3, rd, D), F32), V((rd, D), BF), V((4, rd, D), BF),
            *[V((2, rd // 2, D), BF)] * 4, *[V((rd // 2, D), BF)] * 2, pltpu.SemaphoreType.DMA((10, 2)),
        ]

    def columns(self, s):
        x, x1, x2, x3 = self.chips
        c = jnp.where(s == 0, x2, jnp.where(s == 1, x1, jnp.where(s == 2, x3, x)))
        return pl.ds(pl.multiple_of(c * 2 * self.rd, 128), 2 * self.rd)

    def swap(self, s):
        return remote(self.DS, self.DR.at[s], self.sems.at[s, 0], self.sems.at[s, 1], self.partner)

    def cp(self, which):
        src, dst, dev = self.routes[which]
        return remote(src, dst, self.sems.at[4 + which, 0], self.sems.at[4 + which, 1], dev)

    def compute(self, s, act, rhs):
        rd = self.rd
        self.PT[...] = tn(act[:, self.columns(s)], rhs[...])
        when(s > 0, lambda: self.swap(s - 1).wait_send())
        self.PD[s % 3] = self.PT[tile(self.k, rd), :]
        self.DS[...] = self.PT[tile(1 - self.k, rd), :].astype(BF)
        self.swap(s).start()

    def halve(self, step):
        T, L = self.top, self.low
        self.swap(step).wait_recv()
        v = self.PD[step % 3] + self.DR[step].astype(F32)
        if step == 0:
            self.S1[0], self.S3[0] = v[T].astype(BF), v[L].astype(BF)
            self.cp(0).start()
            self.cp(2).start()
        elif step == 1:
            self.S1[1] = v[T].astype(BF)
            self.cp(1).start()
            self.PD[step, L, :] = v[L]
        elif step == 2:
            self.S3[1] = v[L].astype(BF)
            self.cp(3).start()
            self.PD[step, T, :] = v[T]
        else:
            self.PD[0] = v

    def quarter(self):
        self.cp(0).wait_recv()
        self.cp(2).wait_send()
        self.S3[0] = (self.PD[2, self.top, :] + self.R1[0].astype(F32)).astype(BF)
        self.cp(5).start()
        self.cp(2).wait_recv()
        self.cp(0).wait_send()
        self.S1[0] = (self.PD[1, self.low, :] + self.R3[0].astype(F32)).astype(BF)
        self.cp(4).start()

    def finish(self, layer):
        for which in (1, 3, 4, 5):
            self.cp(which).wait_recv()
        for part, R, Q in ((self.top, self.R1, self.Q3), (self.low, self.R3, self.Q1)):
            g = (self.PD[0, part, :] + R[1].astype(F32) + Q[...].astype(F32)).astype(BF)
            self.GD[layer, part, :] = g
            self.SQ[...] += squares(g)
        self.swap(3).wait_send()
        for which in (1, 3, 4, 5):
            self.cp(which).wait_send()


def first_kernel(a0_ref, dh1_ref, dy_ref, act1_ref, wd0_ref, g0_ref, u0_ref, sq1_ref, gg_in, gu_in,
                 gg_ref, gu_ref, gd_ref, sq_ref,
                 A, DH, WD, ACT, DGU, GT, UT, G, GD, SQ, SQD, TS, TR, local, tsem, gsem, xsem, *scatter):
    T, D = A.shape
    F, TM, n = ACT.shape[1], GT.shape[1], TR.shape[0]
    r, rd, nf, tiles = D // n, F // n, F // CH, T // TM
    split = Scatter.scratch(r)
    s = Scatter(r, scatter[: len(split)], G, SQ, (gg_ref.at[0], gu_ref.at[0]), gsem)
    d = DownScatter(rd, scatter[len(split) :], GD, SQD)
    keep = Local(local)
    dy_in = keep(dy_ref, DH)

    def act_in(step):
        return pltpu.make_async_copy(act1_ref.at[:, d.columns(step)], ACT.at[:, d.columns(step)], tsem.at[2, step])

    for step in range(4):
        act_in(step).start()
    def dh_in(t):
        return pltpu.make_async_copy(dh1_ref.at[tile(t, TM), :], DH.at[tile(t, TM), :], tsem.at[3, t])

    later = [keep(wd0_ref, WD), keep(a0_ref, A)]
    others = [lax.rem(s.me + i, n) for i in range(1, n)]
    meet(others)
    SQ[...] = jnp.zeros_like(SQ)
    SQD[...] = jnp.zeros_like(SQD)

    def fetch(i):
        where = (tile(i % tiles, TM), tile(i // tiles, CH))
        return [pltpu.make_async_copy(ref.at[where], to.at[i % 2], tsem.at[j, i % 2]) for j, (ref, to) in enumerate(((g0_ref, GT), (u0_ref, UT)))]

    for c in fetch(0):
        c.start()
    dy_in.wait()

    @pl.loop(0, 4)
    def _(step):
        act_in(step).wait()
        d.compute(step, ACT, DH)
        for j in range(3):
            when(step == j + 1, lambda: d.halve(j))

    for t in range(tiles):
        dh_in(t).start()
    for c in later:
        c.wait()

    @pl.loop(0, nf)
    def _(f):
        cols = tile(f, CH)

        @pl.loop(0, tiles)
        def _(t):
            i = f * tiles + t

            @pl.when(i + 1 < nf * tiles)
            def _():
                for c in fetch(i + 1):
                    c.start()

            when((t == 0) & (f > 1), lambda: s.quarter(f - 2))
            when((t == 2) & (f > 0), lambda: s.halve(f - 1))
            when((t == 2) & (f == 0), lambda: d.halve(3), d.quarter)
            when(f == 0, dh_in(t).wait)
            for c in fetch(i):
                c.wait()
            for j in range(TM // SUB):
                rows, part = tile(t * (TM // SUB) + j, SUB), pl.ds(j * SUB, SUB)
                dact = nt(DH[rows, :], WD[cols, :]).astype(BF)
                ACT[rows, cols], DGU[rows, :CH], DGU[rows, CH:] = swiglu_back(GT[i % 2, part, :], UT[i % 2, part, :], dact)

        when(f > 1, lambda: s.finish(f - 2))
        s.dot_and_send(f, A[...], DGU[...])
        when(f == 1, lambda: d.finish(1))

    s.quarter(nf - 2)

    @pl.loop(0, 4)
    def _(step):
        d.compute(step, ACT, DH)
        when(step == 0, lambda: s.halve(nf - 1))
        when(step == 1, lambda: s.finish(nf - 2), lambda: d.halve(0))
        when(step == 2, lambda: d.halve(1), lambda: s.quarter(nf - 1))
        when(step == 3, lambda: d.halve(2))

    d.halve(3)
    d.quarter()
    s.finish(nf - 1)
    d.finish(0)
    out = keep(GD, gd_ref)
    TS[...] = jnp.full(TS.shape, jnp.sum(SQ[...]) + jnp.sum(SQD[...]), F32) + sq1_ref[...]
    sums = [remote(TS, TR.at[s.me], xsem.at[0, i], xsem.at[1, s.me], dev) for i, dev in enumerate(others)]
    for c in sums:
        c.start()
    TR[s.me] = TS[...]
    for dev in others:
        remote(TS, TR.at[dev], xsem.at[0, 0], xsem.at[1, dev], others[0]).wait_recv()
    total = TR[0]
    for i in range(1, n):
        total = total + TR[i]
    sq_ref[...] = total
    s.drain(nf - 1)
    for c in sums:
        c.wait_send()
    out.wait()


def adamw(w, m, v, g):
    m = 0.9 * m + 0.1 * g
    v = 0.95 * v + 0.05 * g * g
    step = m * lax.rsqrt(v + 1e-8) + 0.1 * w
    return (w - 0.02 * step).astype(BF), m, v


def solution(mesh):
    n = mesh.shape["dp"]
    ANY, VM = pl.BlockSpec(memory_space=pl.ANY), pl.BlockSpec(memory_space=pltpu.VMEM)
    DMA = pltpu.SemaphoreType.DMA

    def V(*shape, dtype=BF):
        return pltpu.VMEM(shape, dtype)

    def call(body, number, ins, outs, scratch, aliases):
        spec = lambda a: VM if a.shape == (8, 128) else ANY
        return pl.pallas_call(
            body,
            out_shape=outs,
            in_specs=[spec(a) for a in ins],
            out_specs=[spec(a) for a in outs],
            scratch_shapes=scratch,
            input_output_aliases=aliases,
            compiler_params=pltpu.CompilerParams(collective_id=number, has_side_effects=True, vmem_limit_bytes=VMEM_LIMIT),
            name=body.__name__,
        )(*ins)

    def step(x, dy, *arrays):
        (wg, wu, wd), ms, vs = (arrays[i : i + 3] for i in (0, 3, 6))
        x, dy = x[0], dy[0]
        T, D = x.shape
        r, F = wg.shape[1:]
        rd, nf = wd.shape[1], F // CH
        like = jax.ShapeDtypeStruct
        tokens, hidden, wide, down = like((T, D), BF), like((T, F), BF), like((T, F), F32), like((F, D), BF)
        rows, sums = like(wg.shape, BF), like((8, 128), F32)
        TD, DF, FD, TF = V(T, D), V(D, 2 * F), V(F, D), V(T, F)
        gathers = [DMA((2 * nf + 4, 9))] * 2
        G, SQ = V(2, 2, r, CH), V(8, CH, dtype=F32)
        stage = lambda size: [V(2, size, CH, dtype=F32)] * 2
        h1, a0, g0, u0, wd0, wd1 = call(
            forward_kernel, 0, (x, wg, wu, wd), [tokens, tokens, wide, wide, down, down],
            [TD, TD, TF, DF, FD, *stage(CH), DMA((2 * nf + 9,)), DMA((2, 2)), *gathers], {},
        )
        gg, gu, act1, dh1, sq1 = call(
            last_kernel, 1, (h1, dy, wg, wu, wd1), [rows, rows, hidden, tokens, sums],
            [TD, TD, DF, FD, V(T, 2 * F), V(T, CH), G, SQ, DMA((2 * nf + 9,)), DMA((1,)), DMA((2, 2)), *gathers, *Scatter.scratch(r)], {},
        )
        gg, gu, gd, sq = call(
            first_kernel, 2, (a0, dh1, dy, act1, wd0, g0, u0, sq1, gg, gu), [rows, rows, like(wd.shape, BF), sums],
            [TD, TD, FD, TF, V(T, 2 * CH), *stage(CH), G, V(2, rd, D), SQ, V(8, D, dtype=F32), V(8, 128, dtype=F32), V(n, 8, 128, dtype=F32),
             DMA((9,)), DMA((4, 4)), DMA((2, 2)), DMA((2, n)), *Scatter.scratch(r), *DownScatter.scratch(rd, D)],
            {8: 0, 9: 1},
        )
        count = n * (gg.size + gu.size + gd.size)
        factor = jnp.minimum(1.0, 0.5 * lax.rsqrt(sq[0, 0] / count + 1e-30))
        new = [
            adamw(w.astype(F32), m, v, g.astype(F32) * factor)
            for w, m, v, g in zip((wg, wu, wd), ms, vs, (gg, gu, gd), strict=True)
        ]
        return tuple(one[which] for which in range(3) for one in new)

    states, cut = P(("rep", "dp"), None, None), P(None, "dp", None)
    return jax.shard_map(
        step,
        mesh=mesh,
        in_specs=(states, states) + (cut,) * 9,
        out_specs=(P("rep", "dp", None),) * 9,
        check_vma=False,
    )
```

time: 547 us -> 320 us (0.59); the launches traced: 539 us -> 319 us
  Pallas kernels: 0 us -> 302 us
  matrix products: 293 us -> 0 us
  waiting for transfers between devices: 166 us -> 0 us
  local copies, waits for them, and re-layouts: 22 us -> 3 us
  between operations: 17.5 us -> 1.44 us
  blocking collectives: 15.8 us -> 0 us
  other arithmetic: 25 us -> 12.8 us
    pallas_call x0 -> x3, Pallas kernels: none -> 302 us  [call(): pl.pallas_call(body, out_shape=outs, in_specs=[spec(a) for a in ins], out...]
    dot_general x15 -> x0, matrix products: 293 us -> none  [the longest x5 104 us: layer(): gate = jnp.dot(a, w['w_gate'], preferred_element_type=jnp.float32)]
    reduce_scatter x6 -> x0, waiting for transfers between devices: 91.2 us -> none  [step(): lax.psum_scatter(by_w[name], 'dp', scatter_dimension=0, tiled=True)]
    all_gather x6 -> x0, waiting for transfers between devices: 72.3 us -> none  [fetched(): lax.all_gather(w[number], 'dp', axis=0, tiled=True)]
    psum x1 -> x0, blocking collectives: 15.8 us -> none  [step(): squares = lax.psum(sum((jnp.sum(g * g) for g in gradients)), 'dp')]
    unnamed x34 -> x14, local copies, waits for them, and re-layouts: 16.2 us -> 1.81 us
    reduce_sum x4 -> x0, other arithmetic: 10.2 us -> none  [the longest x3 7.43 us: step(): squares = lax.psum(sum((jnp.sum(g * g) for g in gradients)), 'dp')]
  transfers between devices with their start and end apart: 12 -> 0, of which waited for: 9 -> 0; matrix products, arithmetic and copies ran while one was open for 44% -> 0% of each run, Pallas kernels for 0% -> 0%
where the time goes in v1:
time: 320 us; the launch traced here: 319 us
  Pallas kernels  302 us (94%)
  other arithmetic  12.8 us (4%)
    pallas_call x3, Pallas kernels, call(): pl.pallas_call(body, out_shape=outs, in_specs=[spec(a) for a in ins], out...  302 us
    convert_element_type x2, other arithmetic, adamw(): return ((w - 0.02 * step).astype(BF), m, v)  12.8 us

profile of v1, /device:TPU:113, one launch (start us, length us, event | category | flops | bytes accessed | tf_op | source)
XLA Modules:
  0.0 319.4 jit_solution(4679418218463433972)
XLA Ops:
  0.6 86.1 %forward_kernel.1 = (bf16[2048,896]{1,0:T(8,128)(2,1)}, bf16[2048,896]{1,0:T(8,128)(2,1)}, f32[2048,2560]{1,0:T(8,128)}, f32[2048,2560]{1,0:T(8,128)}, bf16[2560...) custom-call(bf16[2048,896]{1,0:T(8,128)(2,1)} %bitcast.5, bf16[2,112,2560]{2,1,0:T(8,128)(2,1)} %wg_ref.3, ...), custom_call_target="tpu_custom_call" | custom-call | tf_op jit(solution)/shard_map/forward_kernel/pallas_call | solution.py:615
  86.8 110.6 %last_kernel.1 = (bf16[2,112,2560]{2,1,0:T(8,128)(2,1)}, bf16[2,112,2560]{2,1,0:T(8,128)(2,1)}, bf16[2048,2560]{1,0:T(8,128)(2,1)}, bf16[2048,896]{1,0:T(8,128)(2,1)}, f32[8,128]{1,0:T(8,128)}) custom-call(bf16[2048,896]{1,0:T(8,128)(2,1)} %get-tuple-element.25.h1_ref, bf16[2048,896]{1,0:T(8,128)(2,1)} %bitcast.3, bf16[2,112,2560]{2,1,0:T(8,128)(2,1)} %wg_ref.3, ...), custom_call_target="tpu_custom_call" | custom-call | tf_op jit(solution)/shard_map/last_kernel/pallas_call | solution.py:615
  197.4 105.5 %first_kernel.1 = (bf16[2,112,2560]{2,1,0:T(8,128)(2,1)}, bf16[2,112,2560]{2,1,0:T(8,128)(2,1)}, bf16[2,320,896]{2,1,0:T(8,128)(2,1)}, f32[8,128]{1,0:T(8,128)}) custom-call(bf16[2048,896]{1,0:T(8,128)(2,1)} %get-tuple-element.24.a0_ref, bf16[2048,896]{1,0:T(8,128)(2,1)} %get-tuple-element.27.dh1_ref, ...), custom_call_target="tpu_custom_call", output_to_operand_aliasing={{0}: (8, {}), {1}: (9, {})} | custom-call | tf_op jit(solution)/shard_map/first_kernel/pallas_call | solution.py:615
  302.9 1.2 slice.3
  304.8 0.0 copy-start
  304.8 0.0 copy-start.1
  304.8 0.0 copy-start.2
  304.8 0.0 copy-start.3
  304.8 0.0 copy-start.4
  304.8 0.0 copy-start.5
  304.8 0.0 copy-start.6
  304.8 6.6 %fusion.8 = (bf16[2,320,896]{2,1,0:T(8,128)(2,1)}, f32[2,320,896]{2,1,0:T(8,128)}, f32[2,320,896]{2,1,0:T(8,128)}) fusion(bf16[2,320,896]{2,1,0:T(8,128)(2,1)} %wd_ref.1, f32[]{:T(128)} %bitcast.2, bf16[2,320,896]{2,1,0:T(8,128)(2,1)} %get-tuple-element.38, f32[2,320,896]{2,1,0:T(8,128)} %param.21, f32[2,320,896]{2,1,0:T(8,128)} %param.18), kind=kLoop, calls=%fused_computation.17 | loop fusion | flops 9748480 | bytes 12615684 | tf_op jit(solution)/shard_map/convert_element_type | solution.py:602
  311.4 0.0 copy-done
  311.4 0.0 copy-done.1
  311.4 0.0 copy-done.2
  311.4 0.0 copy-done.3
  311.4 0.0 copy-done.4
  311.4 1.1 copy-done.5
  312.5 0.7 copy-done.6
  313.2 6.2 %fusion.2 = (bf16[2,112,2560]{2,1,0:T(8,128)(2,1)}, f32[2,112,2560]{2,1,0:T(8,128)}, f32[2,112,2560]{2,1,0:T(8,128)}, bf16[2,112,2560]{2,1,0:T(8,128)(2,1)}, f32...) fusion(bf16[2,112,2560]{2,1,0:T(8,128)(2,1)S(1)} %copy-done, f32[]{:T(128)} %bitcast.2, ...), kind=kLoop, calls=%fused_computation.11 | loop fusion | flops 19496960 | bytes 25231364 | tf_op jit(solution)/shard_map/convert_element_type | solution.py:602
Async XLA Ops:
  304.8 6.6 %copy-start = (bf16[2,112,2560]{2,1,0:T(8,128)(2,1)S(1)}, bf16[2,112,2560]{2,1,0:T(8,128)(2,1)}, u32[]{:S(2)}) copy-start(bf16[2,112,2560]{2,1,0:T(8,128)(2,1)} %wg_ref.3) | copy-start | bytes 3440644
  304.8 6.6 %copy-start.1 = (bf16[2,112,2560]{2,1,0:T(8,128)(2,1)S(1)}, bf16[2,112,2560]{2,1,0:T(8,128)(2,1)}, u32[]{:S(2)}) copy-start(bf16[2,112,2560]{2,1,0:T(8,128)(2,1)} %wu_ref.3) | copy-start | bytes 3440644
  304.8 6.6 %copy-start.2 = (bf16[2,112,2560]{2,1,0:T(8,128)(2,1)S(1)}, bf16[2,112,2560]{2,1,0:T(8,128)(2,1)}, u32[]{:S(2)}) copy-start(bf16[2,112,2560]{2,1,0:T(8,128)(2,1)} %get-tuple-element.35) | copy-start | bytes 3440644
  304.8 6.6 %copy-start.3 = (bf16[2,112,2560]{2,1,0:T(8,128)(2,1)S(1)}, bf16[2,112,2560]{2,1,0:T(8,128)(2,1)}, u32[]{:S(2)}) copy-start(bf16[2,112,2560]{2,1,0:T(8,128)(2,1)} %get-tuple-element.37) | copy-start | bytes 3440644
  304.8 6.6 %copy-start.4 = (f32[2,112,2560]{2,1,0:T(8,128)S(1)}, f32[2,112,2560]{2,1,0:T(8,128)}, u32[]{:S(2)}) copy-start(f32[2,112,2560]{2,1,0:T(8,128)} %param.19) | copy-start | bytes 6881284
  304.8 7.7 %copy-start.5 = (f32[2,112,2560]{2,1,0:T(8,128)S(1)}, f32[2,112,2560]{2,1,0:T(8,128)}, u32[]{:S(2)}) copy-start(f32[2,112,2560]{2,1,0:T(8,128)} %param.16) | copy-start | bytes 6881284
  304.8 8.4 %copy-start.6 = (f32[2,112,2560]{2,1,0:T(8,128)S(1)}, f32[2,112,2560]{2,1,0:T(8,128)}, u32[]{:S(2)}) copy-start(f32[2,112,2560]{2,1,0:T(8,128)} %param.20) | copy-start | bytes 6881284

commit v2 on v1

--- a/solution.py
+++ b/solution.py
@@ -158,8 +158,8 @@
     return [keep(w.at[layer, :, pl.ds(f * CH, CH)], W.at[tile(me, r), pl.ds((2 * f + m) * CH, CH)]) for m, w in enumerate(weights) for f in range(nf)]
 
 
-def forward_kernel(x_ref, wg_ref, wu_ref, wd_ref, h1_ref, a0_ref, g0_ref, u0_ref, wd0_ref, wd1_ref,
-                   X, A, ACT, W, WD, GS, US, local, save, send, recv):
+def forward_kernel(x_ref, wg_ref, wu_ref, wd_ref, h1_ref, a1_ref, a0_ref, g0_ref, u0_ref, wd0_ref, wd1_ref,
+                   X, A, ACT, W, WD, GS, US, local, save, tiled, send, recv):
     T, D = X.shape
     F = ACT.shape[1]
     TM = GS.shape[1]
@@ -225,22 +225,31 @@
     g.pass_on(below)
     g.complete(below)
     out.append(keep(WD, wd0_ref))
+    out.pop(0).wait()
+
+    def h_out(t):
+        rows = tile(t, CH)
+        return [pltpu.make_async_copy(S.at[rows, :], ref.at[rows, :], tiled.at[i, t]) for i, (S, ref) in enumerate(((X, h1_ref), (A, a1_ref)))]
 
     @pl.loop(0, T // CH)
     def _(t):
         rows = tile(t, CH)
         X[rows, :] = (X[rows, :].astype(F32) + nn(ACT[rows, :], WD[...]).astype(BF).astype(F32)).astype(BF)
+        A[rows, :] = normed(X[rows, :])
+        for c in h_out(t):
+            c.start()
         when(t == 0, lambda: g.forward(last[1]))
         when(t == 1, lambda: g.pass_on(last[0]))
         when(t == 2, lambda: g.pass_on(last[1]))
 
-    out.append(keep(X, h1_ref))
     for p in last:
         g.complete(p)
     for p in [chunk(f) for f in range(nf)] + rest:
         g.sent(p)
     for t in range(tiles - 2, tiles):
         out += saving(nf - 1, t)
+    for t in range(T // CH):
+        out += h_out(t)
     for c in out:
         c.wait()
 
@@ -248,7 +257,8 @@
 class Scatter:
     def __init__(self, r, refs, G, SQ, outs, sems):
         self.outs, self.saves = outs, sems
-        self.R, (self.DS, self.DR), (self.AS, self.AR), (self.BS, self.BR), (self.CS, self.CR), (self.ES, self.ER) = refs[0], *zip(refs[1:-1:2], refs[2:-1:2])
+        self.R, (self.DS, self.DR), (self.AS, self.AR), (self.BS, self.BR), (self.CS, self.CR), (self.ES, self.ER) = refs[0], *zip(refs[2:-1:2], refs[3:-1:2])
+        self.Z = refs[1]
         self.r, self.sems, self.G, self.SQ = r, refs[-1], G, SQ
         self.me, self.k, self.chips, (n0, n1, n2, n3), (o0, *_) = place()
         self.routes = ((self.DS, self.DR, o0), (self.AS, self.AR, n1), (self.BS, self.BR, n3), (self.CS, self.CR, n3), (self.ES, self.ER, n1))
@@ -257,7 +267,7 @@
     def scratch(r):
         sent = [(4, r, 2 * CH), (2, r, CH), (2, r, CH), (r, CH), (r, CH)]
         shapes = [s for one in sent for s in (one, (2, *one))]
-        return [pltpu.VMEM((2, 8 * r, 2 * CH), F32), *[pltpu.VMEM(s, BF) for s in shapes], pltpu.SemaphoreType.DMA((5, 3))]
+        return [pltpu.VMEM((2, 8 * r, 2 * CH), F32), pltpu.VMEM((r, 2 * CH), F32), *[pltpu.VMEM(s, BF) for s in shapes], pltpu.SemaphoreType.DMA((5, 3))]
 
     def cp(self, which, f):
         src, dst, dev = self.routes[which]
@@ -294,17 +304,16 @@
         when(f > 0, self.cp(3, f).wait_send, self.cp(4, f).wait_send)
         self.CS[...] = (R[self.rows(3, self.k), :CH] + self.AR[s, 1].astype(F32)).astype(BF)
         self.ES[...] = (R[self.rows(1, self.k), CH:] + self.BR[s, 1].astype(F32)).astype(BF)
+        self.Z[:, :CH] = R[mine, :CH] + self.AR[s, 0].astype(F32)
+        self.Z[:, CH:] = R[mine, CH:] + self.BR[s, 0].astype(F32)
         self.cp(3, f).start()
         self.cp(4, f).start()
-        R[mine, :CH] += self.AR[s, 0].astype(F32)
-        R[mine, CH:] += self.BR[s, 0].astype(F32)
 
     def finish(self, f):
         s = f % 2
         for which in (3, 4):
             self.cp(which, f).wait_recv()
-        v = self.R[s, self.rows(0, self.k), :]
-        for m, (part, last) in enumerate(((v[:, :CH], self.CR), (v[:, CH:], self.ER))):
+        for m, (part, last) in enumerate(((self.Z[:, :CH], self.CR), (self.Z[:, CH:], self.ER))):
             g = (part + last[s].astype(F32)).astype(BF)
             when(f > 1, self.saving(f, m).wait)
             self.G[s, m] = g
@@ -329,7 +338,7 @@
     return (silu * up).astype(BF), (dact * up * (sig + silu * (1.0 - sig))).astype(BF), (dact * silu).astype(BF)
 
 
-def last_kernel(h1_ref, dy_ref, wg_ref, wu_ref, wd1_ref, gg_ref, gu_ref, act1_ref, dh1_ref, sq_ref,
+def last_kernel(h1_ref, a1_ref, dy_ref, wg_ref, wu_ref, wd1_ref, gg_ref, gu_ref, act1_ref, dh1_ref, sq_ref,
                 A, DY, W, WD, DGU, ACT, G, SQ, local, save, gsem, send, recv, *scatter):
     T, D = A.shape
     F = W.shape[1] // 2
@@ -337,16 +346,14 @@
     r, nf, tiles = wg_ref.shape[1], F // CH, T // TM
     g, keep = Gather(send, recv), Local(local)
     s = Scatter(r, scatter, G, SQ, (gg_ref.at[1], gu_ref.at[1]), gsem)
-    h_in, dy_in, wd_in = keep(h1_ref, A), keep(dy_ref, DY), keep(wd1_ref, WD)
-    own = own_rows(keep, 1, r, (wg_ref, wu_ref), W, g.me)
+    first = [keep(dy_ref, DY), keep(wd1_ref, WD)]
+    own = [keep(a1_ref, A)] + own_rows(keep, 1, r, (wg_ref, wu_ref), W, g.me)
     meet(g.partners)
     piece = functools.partial(pair, 1, r, (wg_ref, wu_ref), W)
     g.issue(piece(0))
     SQ[...] = jnp.zeros_like(SQ)
-    h_in.wait()
-    norm_rows(A, A)
-    dy_in.wait()
-    wd_in.wait()
+    for c in first:
+        c.wait()
 
     @pl.loop(0, T // CH)
     def _(t):
@@ -372,7 +379,6 @@
 
         @pl.loop(0, tiles)
         def _(t):
-            when((t == 0) & (f > 1), lambda: s.quarter(f - 2))
             when((t == 0) & (f + 1 < nf), lambda: g.forward(piece(f + 1)))
             when((t == 0) & (f + 3 < nf), lambda: g.issue(piece(f + 3)))
             when((t == 1) & (f > 0), lambda: s.halve(f - 1))
@@ -383,11 +389,15 @@
 
         save_act(f).start()
         when(f + 1 < nf, lambda: g.pass_on(piece(f + 1)))
+        when(f > 1, lambda: s.quarter(f - 2))
+        s.dot_and_send(f, A[...], DGU[:, cols])
         when(f > 1, lambda: s.finish(f - 2))
-        s.dot_and_send(f, A[...], DGU[:, cols])
 
     save_act(nf - 1).wait()
     keep(h1_ref, A).wait()
+
+    def dh_out(t):
+        return pltpu.make_async_copy(DY.at[tile(t, CH), :], dh1_ref.at[tile(t, CH), :], save.at[1 + t])
 
     @pl.loop(0, T // CH)
     def _(t):
@@ -397,17 +407,18 @@
         scale = lax.rsqrt(jnp.mean(wide * wide, -1, keepdims=True) + 1e-6)
         back = (da * scale - wide * (scale * scale * scale * jnp.mean(da * wide, -1, keepdims=True))).astype(BF)
         DY[rows, :] = (DY[rows, :].astype(F32) + back.astype(F32)).astype(BF)
+        dh_out(t).start()
         when(t == 0, lambda: s.quarter(nf - 2), lambda: s.halve(nf - 1))
-        when(t == 1, lambda: s.finish(nf - 2), lambda: s.quarter(nf - 1))
-        when(t == 2, lambda: s.finish(nf - 1))
-
-    out = [keep(DY, dh1_ref)]
+        when(t == 1, lambda: s.finish(nf - 2))
+        when(t == 2, lambda: s.quarter(nf - 1))
+        when(t == 3, lambda: s.finish(nf - 1))
+
     sq_ref[...] = jnp.full(sq_ref.shape, jnp.sum(SQ[...]), F32)
     for f in range(nf):
         g.sent(piece(f))
     s.drain(nf - 1)
-    for c in out:
-        c.wait()
+    for t in range(T // CH):
+        dh_out(t).wait()
 
 
 class DownScatter:
@@ -595,11 +606,35 @@
     out.wait()
 
 
-def adamw(w, m, v, g):
-    m = 0.9 * m + 0.1 * g
-    v = 0.95 * v + 0.05 * g * g
-    step = m * lax.rsqrt(v + 1e-8) + 0.1 * w
-    return (w - 0.02 * step).astype(BF), m, v
+def adamw_kernel(count, sq_ref, *refs):
+    factor = jnp.minimum(1.0, 0.5 * lax.rsqrt(sq_ref[:1, :1] / count + 1e-30))
+    for i in range(3):
+        w, m, v, g, new_w, new_m, new_v = (refs[j][0] if j < 12 else refs[j] for j in range(i, 21, 3))
+        w, g = w.astype(F32), g.astype(F32) * factor
+        m = 0.9 * m + 0.1 * g
+        v = 0.95 * v + 0.05 * g * g
+        step = m * lax.rsqrt(v + 1e-8) + 0.1 * w
+        new_w[0], new_m[0], new_v[0] = (w - 0.02 * step).astype(BF), m, v
+
+
+def adamw(sq, count, weights, ms, vs, gradients):
+    blocks = 4
+    arrays = (*weights, *ms, *vs, *gradients)
+
+    def spec(a):
+        layers, rows, cols = a.shape
+        if rows < cols // blocks:
+            return pl.BlockSpec((1, rows, cols // blocks), lambda i, j: (i, 0, j))
+        return pl.BlockSpec((1, rows // blocks, cols), lambda i, j: (i, j, 0))
+
+    return pl.pallas_call(
+        functools.partial(adamw_kernel, count),
+        grid=(weights[0].shape[0], blocks),
+        out_shape=[jax.ShapeDtypeStruct(a.shape, a.dtype) for a in arrays[:9]],
+        in_specs=[pl.BlockSpec(sq.shape, lambda i, j: (0, 0)), *map(spec, arrays)],
+        out_specs=[*map(spec, arrays[:9])],
+        name="adamw",
+    )(sq, *arrays)
 
 
 def solution(mesh):
@@ -636,13 +671,13 @@
         gathers = [DMA((2 * nf + 4, 9))] * 2
         G, SQ = V(2, 2, r, CH), V(8, CH, dtype=F32)
         stage = lambda size: [V(2, size, CH, dtype=F32)] * 2
-        h1, a0, g0, u0, wd0, wd1 = call(
-            forward_kernel, 0, (x, wg, wu, wd), [tokens, tokens, wide, wide, down, down],
-            [TD, TD, TF, DF, FD, *stage(CH), DMA((2 * nf + 9,)), DMA((2, 2)), *gathers], {},
+        h1, a1, a0, g0, u0, wd0, wd1 = call(
+            forward_kernel, 0, (x, wg, wu, wd), [tokens, tokens, tokens, wide, wide, down, down],
+            [TD, TD, TF, DF, FD, *stage(CH), DMA((2 * nf + 9,)), DMA((2, 2)), DMA((2, T // CH)), *gathers], {},
         )
         gg, gu, act1, dh1, sq1 = call(
-            last_kernel, 1, (h1, dy, wg, wu, wd1), [rows, rows, hidden, tokens, sums],
-            [TD, TD, DF, FD, V(T, 2 * F), V(T, CH), G, SQ, DMA((2 * nf + 9,)), DMA((1,)), DMA((2, 2)), *gathers, *Scatter.scratch(r)], {},
+            last_kernel, 1, (h1, a1, dy, wg, wu, wd1), [rows, rows, hidden, tokens, sums],
+            [TD, TD, DF, FD, V(T, 2 * F), V(T, CH), G, SQ, DMA((2 * nf + 9,)), DMA((1 + T // CH,)), DMA((2, 2)), *gathers, *Scatter.scratch(r)], {},
         )
         gg, gu, gd, sq = call(
             first_kernel, 2, (a0, dh1, dy, act1, wd0, g0, u0, sq1, gg, gu), [rows, rows, like(wd.shape, BF), sums],
@@ -650,13 +685,7 @@
              DMA((9,)), DMA((4, 4)), DMA((2, 2)), DMA((2, n)), *Scatter.scratch(r), *DownScatter.scratch(rd, D)],
             {8: 0, 9: 1},
         )
-        count = n * (gg.size + gu.size + gd.size)
-        factor = jnp.minimum(1.0, 0.5 * lax.rsqrt(sq[0, 0] / count + 1e-30))
-        new = [
-            adamw(w.astype(F32), m, v, g.astype(F32) * factor)
-            for w, m, v, g in zip((wg, wu, wd), ms, vs, (gg, gu, gd), strict=True)
-        ]
-        return tuple(one[which] for which in range(3) for one in new)
+        return tuple(adamw(sq, n * (gg.size + gu.size + gd.size), (wg, wu, wd), ms, vs, (gg, gu, gd)))
 
     states, cut = P(("rep", "dp"), None, None), P(None, "dp", None)
     return jax.shard_map(

time: 320 us -> 315 us (0.984)
  other arithmetic: 12.8 us -> 0 us
  Pallas kernels: 302 us -> 314 us
    pallas_call x0 -> x1, Pallas kernels: none -> 15 us  [adamw(): pl.pallas_call(functools.partial(adamw_kernel, count), grid=(weights[0].s...]
    convert_element_type x2 -> x0, other arithmetic: 12.8 us -> none  [adamw(): return ((w - 0.02 * step).astype(BF), m, v)]
    pallas_call x3, Pallas kernels: 302 us -> 299 us  [call(): pl.pallas_call(body, out_shape=outs, in_specs=[spec(a) for a in ins], out...]
where the time goes in v2:
time: 315 us
  Pallas kernels  314 us (100%)
    pallas_call x3, Pallas kernels, call(): pl.pallas_call(body, out_shape=outs, in_specs=[spec(a) for a in ins], out...  299 us
    pallas_call x1, Pallas kernels, adamw(): pl.pallas_call(functools.partial(adamw_kernel, count), grid=(weights[0].s...  15 us

profile of v2, /device:TPU:113, one launch (start us, length us, event | category | flops | bytes accessed | tf_op | source)
XLA Modules:
  0.0 314.6 jit_solution(1259807194649455855)
XLA Ops:
  0.6 85.7 %forward_kernel.1 = (bf16[2048,896]{1,0:T(8,128)(2,1)}, bf16[2048,896]{1,0:T(8,128)(2,1)}, bf16[2048,896]{1,0:T(8,128)(2,1)}, f32[2048,2560]{1,0:T(8,128)}, f32[...) custom-call(bf16[2048,896]{1,0:T(8,128)(2,1)} %bitcast.4, bf16[2,112,2560]{2,1,0:T(8,128)(2,1)} %refs_0_.1, ...), custom_call_target="tpu_custom_call" | custom-call | tf_op jit(solution)/shard_map/forward_kernel/pallas_call | solution.py:650
  86.3 107.7 %last_kernel.1 = (bf16[2,112,2560]{2,1,0:T(8,128)(2,1)}, bf16[2,112,2560]{2,1,0:T(8,128)(2,1)}, bf16[2048,2560]{1,0:T(8,128)(2,1)}, bf16[2048,896]{1,0:T(8,128)(2,1)}, f32[8,128]{1,0:T(8,128)}) custom-call(bf16[2048,896]{1,0:T(8,128)(2,1)} %get-tuple-element.26.h1_ref, bf16[2048,896]{1,0:T(8,128)(2,1)} %get-tuple-element.27.a1_ref, ...), custom_call_target="tpu_custom_call" | custom-call | tf_op jit(solution)/shard_map/last_kernel/pallas_call | solution.py:650
  194.0 105.5 %first_kernel.1 = (bf16[2,112,2560]{2,1,0:T(8,128)(2,1)}, bf16[2,112,2560]{2,1,0:T(8,128)(2,1)}, bf16[2,320,896]{2,1,0:T(8,128)(2,1)}, f32[8,128]{1,0:T(8,128)}) custom-call(bf16[2048,896]{1,0:T(8,128)(2,1)} %get-tuple-element.25.a0_ref, bf16[2048,896]{1,0:T(8,128)(2,1)} %get-tuple-element.29.dh1_ref, ...), custom_call_target="tpu_custom_call", output_to_operand_aliasing={{0}: (8, {}), {1}: (9, {})} | custom-call | tf_op jit(solution)/shard_map/first_kernel/pallas_call | solution.py:650
  299.5 15.0 %adamw.1 = (bf16[2,112,2560]{2,1,0:T(8,128)(2,1)}, bf16[2,112,2560]{2,1,0:T(8,128)(2,1)}, bf16[2,320,896]{2,1,0:T(8,128)(2,1)}, f32[2,112,2560]{2,1,0:T(8,128)},...) custom-call(f32[8,128]{1,0:T(8,128)} %get-tuple-element.37.sq_ref, ...), custom_call_target="tpu_custom_call" | custom-call | tf_op jit(solution)/shard_map/adamw/pallas_call | solution.py:630
